TPU v7x, 16 devices: a 4x2x1 block of a 4x4x8 slice. The times are simulated.
16 devices in a mesh: rep: 4 (over y, z, core), dp: 4 (over x).
Axes of the slice: x: 4, y: 2, z: 1, core: 2. Of those that a mesh axis runs over, the one named last changes fastest.
The devices are a block of a 4x4x8 slice.
Arguments:
- g_w_gate: bfloat16 [16, 2, 1024, 4096], P(('rep', 'dp')), parts along dimension 0
- g_w_up: bfloat16 [16, 2, 1024, 4096], P(('rep', 'dp')), parts along dimension 0
- g_w_down: bfloat16 [16, 2, 4096, 1024], P(('rep', 'dp')), parts along dimension 0
- w_gate: bfloat16 [2, 1024, 4096], replicated
- w_up: bfloat16 [2, 1024, 4096], replicated
- w_down: bfloat16 [2, 4096, 1024], replicated
- m_w_gate: float32 [2, 1024, 4096], P(None, 'dp')
- m_w_up: float32 [2, 1024, 4096], P(None, 'dp')
- m_w_down: float32 [2, 4096, 1024], P(None, 'dp')
- v_w_gate: float32 [2, 1024, 4096], P(None, 'dp')
- v_w_up: float32 [2, 1024, 4096], P(None, 'dp')
- v_w_down: float32 [2, 4096, 1024], P(None, 'dp')
Outputs:
- output 1: bfloat16 [8, 1024, 4096], P('rep'), parts along dimension 0
- output 2: bfloat16 [8, 1024, 4096], P('rep'), parts along dimension 0
- output 3: bfloat16 [8, 4096, 1024], P('rep'), parts along dimension 0
- output 4: float32 [8, 1024, 4096], P('rep', 'dp'), parts along dimension 0
- output 5: float32 [8, 1024, 4096], P('rep', 'dp'), parts along dimension 0
- output 6: float32 [8, 4096, 1024], P('rep', 'dp'), parts along dimension 0
- output 7: float32 [8, 1024, 4096], P('rep', 'dp'), parts along dimension 0
- output 8: float32 [8, 1024, 4096], P('rep', 'dp'), parts along dimension 0
- output 9: float32 [8, 4096, 1024], P('rep', 'dp'), parts along dimension 0
There are 4 independent parts. A program takes and returns all parts, laid end to end along the dimension named above; an argument that names none is the same for every part.
All inputs are finite; a program needn't handle non-finite values.
Results may differ from a plain program's by a relative error of at most 0.022.
Values are sent between devices in bfloat16 or wider.
A program may use at most 768 MiB of HBM per device.

v0:
```python
import functools

import jax
import jax.numpy as jnp
from jax import lax
from jax.experimental import pallas as pl
from jax.experimental.pallas import tpu as pltpu
from jax.sharding import PartitionSpec as P


MESH = pl.DeviceIdType.MESH
ROWS, COLS = 256, 1024
RIGHT, LEFT = 0, 1
STRIP = 32
LATER = 4
LAST = 1
PAUSE = 96
FLIGHT = 32
VMEM_LIMIT = 67043328


def adamw(w, m, v, g):
    m = 0.9 * m + 0.1 * g
    v = 0.95 * v + 0.05 * g * g
    step = m * lax.rsqrt(v + 1e-8) + 0.1 * w
    return (w - 0.02 * step).astype(jnp.bfloat16), m, v


class Lay:
    def __init__(self, block):
        self.layers, self.rows, self.cols = block
        self.across = self.cols // COLS
        tiles = (self.rows // ROWS) * self.across
        assert self.rows % ROWS == 0 and self.cols % COLS == 0 and tiles % 2 == 0
        assert self.across == 1 or self.rows == ROWS
        self.tiles = tiles // 2
        self.half = (self.rows // 2, self.cols) if self.across == 1 else (self.rows, self.cols // 2)

    def of(self, ref, layer, owner, h):
        down, over = (h, 0) if self.across == 1 else (0, h)
        start = pl.multiple_of(owner * self.rows + down * self.half[0], ROWS)
        return ref.at[layer, pl.ds(start, self.half[0]), pl.ds(over * self.half[1], self.half[1])]

    def whole(self, ref, layer, owner):
        return ref.at[layer, pl.ds(pl.multiple_of(owner * self.rows, ROWS), self.rows)]

    def tile(self, ref, layer, owner, h, t):
        q = h * self.tiles + t
        start = pl.multiple_of(owner * self.rows + (q // self.across) * ROWS, ROWS)
        return ref.at[layer, pl.ds(start, ROWS), pl.ds((q % self.across) * COLS, COLS)]

    def inside(self, t, strip):
        down, over = (t, 0) if self.across == 1 else (0, t)
        if strip is None:
            return pl.ds(down * ROWS, ROWS), pl.ds(over * COLS, COLS)
        return pl.ds(pl.multiple_of(down * ROWS + strip * STRIP, STRIP), STRIP), pl.ds(over * COLS, COLS)


def kernel(lay, *refs):
    grads, weights, ms, vs, sums, gathered = (refs[i : i + 3] for i in range(0, 18, 3))
    onward, hop, got = refs[18:22], refs[22:25], refs[25:28]
    (
        own_b, g_b, w_b, m_b, v_b, sum_b, new_b,
        s1_send, s1_recv, s2_send, s2_recv, a1_send, a1_recv, a2_send, a2_recv,
        own_sem, in_sem, out_sem, put_sem,
    ) = refs[28:]
    n = lax.axis_size("dp")
    me = lax.axis_index("dp")
    rep = lax.axis_index("rep")
    right, left, across = lax.rem(me + 1, n), lax.rem(me + n - 1, n), lax.rem(me + 2, n)
    to = (right, left)
    came = (left, right)
    units = [(i, layer) for i in range(3) for layer in range(lay[i].layers)]
    many = range(len(units))
    tiles = lay[0].tiles
    ways = (RIGHT, LEFT)

    def remote(src, dst, sends, recvs, d, k):
        return pltpu.make_async_remote_copy(
            src_ref=src,
            dst_ref=dst,
            send_sem=sends.at[d, k],
            recv_sem=recvs.at[d, k],
            device_id=(rep, to[d]),
            device_id_type=MESH,
        )

    def part(arrays, u, owner, h):
        i, layer = units[u]
        return lay[i].of(arrays[i], layer, owner, h)

    def tile(arrays, u, owner, h, t):
        i, layer = units[u]
        return lay[i].tile(arrays[i], layer, owner, h, t)

    def first(d, i):
        return remote(lay[i].of(grads[i], slice(None), across, d), hop[i].at[d], s1_send, s1_recv, d, i)

    def plain(d, i):
        src = lay[i].of(grads[i], slice(None), to[d], 1 - d)
        return remote(src, got[i].at[d, 1 - d], s2_send, s2_recv, d, 2 * i + 1 - d)

    def added(d, i):
        return remote(hop[i].at[d], got[i].at[d, d], s2_send, s2_recv, d, 2 * i + d)

    def out(d, u):
        i, layer = units[u]
        src = lay[i].whole(gathered[i], layer, me)
        return remote(src, src, a1_send, a1_recv, d, u)

    def on(d, u):
        src = part(gathered, u, came[d], d)
        return remote(src, src, a2_send, a2_recv, d, u)

    barrier = pltpu.get_barrier_semaphore()
    for device in to:
        pl.semaphore_signal(barrier, inc=1, device_id=(rep, device), device_id_type=MESH)

    adds = [(d, u, t) for i in range(3) for d in ways for u in many if units[u][0] == i for t in range(tiles)]
    steps = [(u, h, t) for u in many for h in range(2) for t in range(tiles)]

    def own_load(k):
        d, u, t = adds[k]
        return pltpu.make_async_copy(tile(grads, u, to[d], d, t), own_b.at[k % 2], own_sem.at[k % 2])

    def loads(k):
        u, h, t = steps[k]
        s = k % 2
        pairs = ((tile(grads, u, me, h, t), g_b), (tile(weights, u, me, h, t), w_b), (tile(ms, u, 0, h, t), m_b), (tile(vs, u, 0, h, t), v_b))
        return [pltpu.make_async_copy(src, dst.at[s], in_sem.at[a, s]) for a, (src, dst) in enumerate(pairs)]

    def store_new(k):
        u, h, t = steps[k]
        return pltpu.make_async_copy(new_b.at[k % 2], tile(gathered, u, me, h, t), out_sem.at[0, k % 2])

    def store_sum(k):
        u, h, t = steps[k]
        return pltpu.make_async_copy(sum_b.at[k % 2], tile(sums, u, 0, h, t), out_sem.at[1, k % 2])

    own_load(0).start()
    for copy in loads(0):
        copy.start()

    pl.semaphore_wait(barrier, 2)

    @pl.when(lax.rem(rep, 2) == 0)
    def _():
        @pl.loop(0, PAUSE * (ROWS // STRIP))
        def _(turn):
            at = pl.ds(pl.multiple_of(lax.rem(turn, ROWS // STRIP) * STRIP, STRIP), STRIP)
            m_b[1, at, :] = jnp.zeros((STRIP, COLS), jnp.float32)

    for i in range(3):
        for d in ways:
            first(d, i).start()
    for i in range(3):
        for d in ways:
            plain(d, i).start()

    for k, (d, u, t) in enumerate(adds):
        i, layer = units[u]
        if k + 1 < len(adds):
            own_load(k + 1).start()
        own_load(k).wait()
        if layer == t == 0:
            first(d, i).wait_recv()

        @pl.loop(0, ROWS // STRIP)
        def _(strip, d=d, i=i, layer=layer, t=t, k=k):
            at = pl.ds(pl.multiple_of(strip * STRIP, STRIP), STRIP)
            there = (d, layer, *lay[i].inside(t, strip))
            hop[i][there] = (hop[i][there].astype(jnp.float32) + own_b[k % 2, at, :].astype(jnp.float32)).astype(jnp.bfloat16)

        if layer == lay[i].layers - 1 and t == tiles - 1:
            added(d, i).start()

    def send_out(k):
        u, h, t = steps[k]
        store_new(k).wait()
        if h == 1 and t == tiles - 1:
            for d in ways:
                out(d, u).start()

    for k, (u, h, t) in enumerate(steps):
        s = k % 2
        i, layer = units[u]
        if k + 1 < len(steps):
            for copy in loads(k + 1):
                copy.start()
        for copy in loads(k):
            copy.wait()
        if layer == t == 0:
            for d in ways:
                (added if d == h else plain)(d, i).wait_recv()
        if k >= 2:
            store_sum(k - 2).wait()

        @pl.loop(0, ROWS // STRIP)
        def _(strip, s=s, i=i, layer=layer, h=h, t=t):
            at = pl.ds(pl.multiple_of(strip * STRIP, STRIP), STRIP)
            there = (h, layer, *lay[i].inside(t, strip))
            g = g_b[s, at, :].astype(jnp.float32) + got[i][(RIGHT, *there)].astype(jnp.float32)
            g = (g + got[i][(LEFT, *there)].astype(jnp.float32)).astype(jnp.bfloat16)
            sum_b[s, at, :] = g
            new_b[s, at, :] = adamw(w_b[s, at, :].astype(jnp.float32), m_b[s, at, :], v_b[s, at, :], g.astype(jnp.float32))[0]

        store_new(k).start()
        store_sum(k).start()
        if k >= 1:
            send_out(k - 1)
    end = len(steps) - 1
    send_out(end)
    store_sum(end - 1).wait()
    store_sum(end).wait()

    split = LATER * tiles - LAST
    later = [(u, d) for u in range(LATER) for d in ways]

    def take(k):
        u, d = later[k]
        i, layer = units[u]
        return pltpu.make_async_copy(part(gathered, u, came[d], d), hop[i].at[d, layer], own_sem.at[k % 2])

    def put(k, t):
        u, d = later[k]
        i, layer = units[u]
        src = hop[i].at[(d, layer, *lay[i].inside(t, None))]
        to_k = u * tiles + t
        dst = onward[d].at[to_k] if to_k < split else onward[2 + d].at[to_k - split]
        return pltpu.make_async_copy(src, dst, put_sem.at[k % 2, t])

    for i in range(3):
        for d in ways:
            added(d, i).wait_send()
    for k in range(len(later) + 2):
        if k < len(later):
            u, d = later[k]
            out(d, u).wait_recv()
            take(k).start()
        if 1 <= k <= len(later):
            take(k - 1).wait()
            for t in range(tiles):
                put(k - 1, t).start()
        if k >= 2:
            for t in range(tiles):
                put(k - 2, t).wait()
    for u in many[LATER:]:
        for d in ways:
            out(d, u).wait_recv()
            on(d, u).start()

    for d in ways:
        for i in range(3):
            first(d, i).wait_send()
            plain(d, i).wait_send()
        for u in many:
            out(d, u).wait_send()
            if u >= LATER:
                on(d, u).wait()


def settle(lay, *refs):
    ins, outs, buf, in_sem, out_sem = refs[:3], refs[3:6], refs[6], refs[7], refs[8]
    n = lax.axis_size("dp")
    me = lax.axis_index("dp")
    units = [(i, layer) for i in range(3) for layer in range(lay[i].layers)]
    tiles = [
        (i, layer, lax.rem(me + hops, n), h, t)
        for u, (i, layer) in enumerate(units)
        for hops in range(4)
        for h in range(2)
        for t in range(lay[i].tiles)
        if hops != 2 or u >= LATER
    ]

    def take(k):
        i, *where = tiles[k]
        return pltpu.make_async_copy(lay[i].tile(ins[i], *where), buf.at[k % FLIGHT], in_sem.at[k % FLIGHT])

    def put(k):
        i, *where = tiles[k]
        return pltpu.make_async_copy(buf.at[k % FLIGHT], lay[i].tile(outs[i], *where), out_sem.at[k % FLIGHT])

    lag = FLIGHT // 2
    for k in range(len(tiles) + lag):
        if k < len(tiles):
            if k >= FLIGHT:
                put(k - FLIGHT).wait()
            take(k).start()
        if k >= lag:
            take(k - lag).wait()
            put(k - lag).start()
    for k in range(len(tiles) - FLIGHT, len(tiles)):
        put(k).wait()


def spread(lay, first, *refs):
    brought, outs, sem = refs[:2], refs[5:8], refs[8]
    n = lax.axis_size("dp")
    across = lax.rem(lax.axis_index("dp") + 2, n)
    units = [(i, layer) for i in range(3) for layer in range(lay[i].layers)]
    tiles = lay[0].tiles
    copies = []
    for d in (RIGHT, LEFT):
        for k in range(brought[d].shape[0]):
            i, layer = units[(first + k) // tiles]
            dst = lay[i].tile(outs[i], layer, across, d, (first + k) % tiles)
            copies.append(pltpu.make_async_copy(brought[d].at[k], dst, sem.at[len(copies)]))
    for copy in copies:
        copy.start()
    for copy in copies:
        copy.wait()


def solution(mesh):
    def step(*arrays):
        terms, weights, m, v = (arrays[i : i + 3] for i in (0, 3, 6, 9))
        lay = [Lay(one.shape) for one in m]
        tiles = lay[0].tiles
        assert all(one.tiles == tiles for one in lay) and mesh.shape["dp"] == 4
        units = sum(one.layers for one in lay)
        anywhere = pl.BlockSpec(memory_space=pl.ANY)
        bf16 = jnp.bfloat16
        dma = pltpu.SemaphoreType.DMA
        res = pl.pallas_call(
            functools.partial(kernel, lay),
            out_shape=[jax.ShapeDtypeStruct(one.shape, bf16) for one in m]
            + [jax.ShapeDtypeStruct(one.shape, bf16) for one in weights]
            + [jax.ShapeDtypeStruct((LATER * tiles - LAST, ROWS, COLS), bf16)] * 2
            + [jax.ShapeDtypeStruct((LAST, ROWS, COLS), bf16)] * 2,
            in_specs=[anywhere] * 12,
            out_specs=[anywhere] * 10,
            scratch_shapes=[
                *(pltpu.VMEM((2, one.layers, *one.half), bf16) for one in lay),
                *(pltpu.VMEM((2, 2, one.layers, *one.half), bf16) for one in lay),
                pltpu.VMEM((2, ROWS, COLS), bf16),
                pltpu.VMEM((2, ROWS, COLS), bf16),
                pltpu.VMEM((2, ROWS, COLS), bf16),
                pltpu.VMEM((2, ROWS, COLS), jnp.float32),
                pltpu.VMEM((2, ROWS, COLS), jnp.float32),
                pltpu.VMEM((2, ROWS, COLS), bf16),
                pltpu.VMEM((2, ROWS, COLS), bf16),
                dma((2, 3)), dma((2, 3)),
                dma((2, 6)), dma((2, 6)),
                dma((2, units)), dma((2, units)),
                dma((2, units)), dma((2, units)),
                dma((2,)), dma((4, 2)), dma((2, 2)), dma((2, tiles)),
            ],
            compiler_params=pltpu.CompilerParams(collective_id=0, has_side_effects=True, vmem_limit_bytes=VMEM_LIMIT),
            name="sum_step_gather",
        )(*(t[0] for t in terms), *weights, *m, *v)
        sums, gathered, onward = res[:3], res[3:6], res[6:10]
        n = mesh.shape["dp"]
        brought = []
        for k in (0, 2):
            for x, hop in zip(onward[k : k + 2], (1, -1), strict=True):
                brought.append(lax.ppermute(x, "dp", [(i, (i + hop) % n) for i in range(n)]))
        size = sum(one.size for one in gathered)
        wholes = pl.pallas_call(
            functools.partial(settle, lay),
            out_shape=[jax.ShapeDtypeStruct(one.shape, one.dtype) for one in gathered],
            in_specs=[anywhere] * 3,
            out_specs=[anywhere] * 3,
            scratch_shapes=[pltpu.VMEM((FLIGHT, ROWS, COLS), bf16), dma((FLIGHT,)), dma((FLIGHT,))],
            compiler_params=pltpu.CompilerParams(vmem_limit_bytes=54 << 20),
            cost_estimate=pl.CostEstimate(flops=size * 40, bytes_accessed=4 * size, transcendentals=0),
            name="settle",
        )(*gathered)
        new_m, new_v = [], []
        for one_m, one_v, g in zip(m, v, sums, strict=True):
            g = g.astype(jnp.float32)
            new_m.append(0.9 * one_m + 0.1 * g)
            new_v.append(0.95 * one_v + 0.05 * g * g)
        for pair, first in ((brought[:2], 0), (brought[2:], LATER * tiles - LAST)):
            wholes = pl.pallas_call(
                functools.partial(spread, lay, first),
                out_shape=[jax.ShapeDtypeStruct(one.shape, one.dtype) for one in wholes],
                in_specs=[pl.BlockSpec(memory_space=pltpu.VMEM)] * 2 + [anywhere] * 3,
                out_specs=[anywhere] * 3,
                input_output_aliases={2: 0, 3: 1, 4: 2},
                scratch_shapes=[dma((2 * pair[0].shape[0],))],
                compiler_params=pltpu.CompilerParams(vmem_limit_bytes=24 << 20),
                name="spread",
            )(*pair, *wholes)
        return (*wholes, *new_m, *new_v)

    all_of, cut = P(None, None, None), P(None, "dp", None)
    return jax.shard_map(
        step,
        mesh=mesh,
        in_specs=(P(("rep", "dp"), None, None, None),) * 3 + (all_of,) * 3 + (cut,) * 6,
        out_specs=(P("rep", None, None),) * 3 + (P("rep", "dp", None),) * 6,
        check_vma=False,
    )
```

profile of v0, /device:TPU:112, one launch (start us, length us, event | category | flops | bytes accessed | tf_op | source)
XLA Modules:
  0.0 815.9 jit_solution(7557417122217779747)
XLA Ops:
  0.6 731.4 %sum_step_gather.1 = (bf16[2,256,4096]{2,1,0:T(8,128)(2,1)}, bf16[2,256,4096]{2,1,0:T(8,128)(2,1)}, bf16[2,1024,1024]{2,1,0:T(8,128)(2,1)}, bf16[2,1024,4096]{2,...) custom-call(bf16[2,1024,4096]{2,1,0:T(8,128)(2,1)} %bitcast.3, ...), custom_call_target="tpu_custom_call" | custom-call | tf_op jit(solution)/shard_map/sum_step_gather/pallas_call | solution.py:325
  732.1 2.6 collective-permute-start.2
  734.6 0.8 collective-permute-start.3
  735.4 1.3 collective-permute-start
  736.7 2.0 collective-permute-start.1
  738.6 0.0 copy-start
  738.6 26.4 %fusion.3 = (f32[2,256,4096]{2,1,0:T(8,128)}, f32[2,256,4096]{2,1,0:T(8,128)}, f32[2,256,4096]{2,1,0:T(8,128)}, f32[2,256,4096]{2,1,0:T(8,128)}) fusion(bf16[2,256,4096]{2,1,0:T(8,128)(2,1)} %get-tuple-element.44, f32[2,256,4096]{2,1,0:T(8,128)} %refs_9_.1, f32[2,256,4096]{2,1,0:T(8,128)} %refs_6_.1, bf16[2,256,4096]{2,1,0:T(8,128)(2,1)} %get-tuple-element.45, ...), kind=kLoop, calls=%fused_computation.9 | loop fusion | flops 33554432 | bytes 75497472 | tf_op jit(solution)/shard_map/add | solution.py:373
  765.0 0.0 copy-done
  765.1 10.4 %fusion.5 = (f32[2,1024,1024]{2,1,0:T(8,128)}, f32[2,1024,1024]{2,1,0:T(8,128)}) fusion(bf16[2,1024,1024]{2,1,0:T(8,128)(2,1)} %get-tuple-element.46, f32[2,1024,1024]{2,1,0:T(8,128)} %refs_11_.1, f32[2,1024,1024]{2,1,0:T(8,128)S(1)} %copy-done), kind=kLoop, calls=%fused_computation.11 | loop fusion | flops 16777216 | bytes 37748736 | tf_op jit(solution)/shard_map/add | solution.py:373
  775.5 27.9 %settle.1 = (bf16[2,1024,4096]{2,1,0:T(8,128)(2,1)}, bf16[2,1024,4096]{2,1,0:T(8,128)(2,1)}, bf16[2,4096,1024]{2,1,0:T(8,128)(2,1)}) custom-call(bf16[2,1024,4096]{2,1,0:T(8,128)(2,1)} %get-tuple-element.32.refs_0_, bf16[2,1024,4096]{2,1,0:T(8,128)(2,1)} %get-tuple-element.33.refs_1_, bf16[2,4096,1024]{2,1,0:T(8,128)(2,1)} %get-tuple-element.34.refs_2_), custom_call_target="tpu_custom_call" | custom-call | flops 1006632960 | bytes 100663296 | tf_op jit(solution)/shard_map/settle/pallas_call | solution.py:359
  803.3 6.0 collective-permute-done.2.refs_0_
  809.3 0.0 collective-permute-done.3.refs_1_
  809.3 3.1 spread.2
  812.4 2.5 collective-permute-done.refs_0_
  814.9 0.0 collective-permute-done.1.refs_1_
  814.9 1.0 spread.3
Async XLA Ops:
  732.1 77.2 %collective-permute-start.2 = (bf16[7,256,1024]{2,1,0:T(8,128)(2,1)}, bf16[7,256,1024]{2,1,0:T(8,128)(2,1)S(1)}, u32[]{:S(2)}, u32[]{:S(2)}) collective-permute-start(bf16[7,256,1024]{2,1,0:T(8,128)(2,1)} %get-tuple-element.30), channel_id=1, source_target_pairs={{0,1},{1,2},{2,3},{3,0},{4,5},{5,6},{6,7},{7,4},{8,9},{9,10},{10,1... | collective-permute-start | bytes 11010056 | tf_op jit(solution)/shard_map/ppermute | solution.py:357
  734.6 74.7 %collective-permute-start.3 = (bf16[7,256,1024]{2,1,0:T(8,128)(2,1)}, bf16[7,256,1024]{2,1,0:T(8,128)(2,1)S(1)}, u32[]{:S(2)}, u32[]{:S(2)}) collective-permute-start(bf16[7,256,1024]{2,1,0:T(8,128)(2,1)} %get-tuple-element.31), channel_id=1, source_target_pairs={{0,3},{1,0},{2,1},{3,2},{4,7},{5,4},{6,5},{7,6},{8,11},{9,8},{10,9... | collective-permute-start | bytes 11010056 | tf_op jit(solution)/shard_map/ppermute | solution.py:357
  735.4 79.5 %collective-permute-start = (bf16[1,256,1024]{2,1,0:T(8,128)(2,1)}, bf16[1,256,1024]{2,1,0:T(8,128)(2,1)S(1)}, u32[]{:S(2)}, u32[]{:S(2)}) collective-permute-start(bf16[1,256,1024]{2,1,0:T(8,128)(2,1)} %get-tuple-element.28), channel_id=1, source_target_pairs={{0,1},{1,2},{2,3},{3,0},{4,5},{5,6},{6,7},{7,4},{8,9},{9,10},{10,1... | collective-permute-start | bytes 1572872 | tf_op jit(solution)/shard_map/ppermute | solution.py:357
  736.7 78.3 %collective-permute-start.1 = (bf16[1,256,1024]{2,1,0:T(8,128)(2,1)}, bf16[1,256,1024]{2,1,0:T(8,128)(2,1)S(1)}, u32[]{:S(2)}, u32[]{:S(2)}) collective-permute-start(bf16[1,256,1024]{2,1,0:T(8,128)(2,1)} %get-tuple-element.29), channel_id=1, source_target_pairs={{0,3},{1,0},{2,1},{3,2},{4,7},{5,4},{6,5},{7,6},{8,11},{9,8},{10,9... | collective-permute-start | bytes 1572872 | tf_op jit(solution)/shard_map/ppermute | solution.py:357
  738.6 26.4 %copy-start = (f32[2,1024,1024]{2,1,0:T(8,128)S(1)}, f32[2,1024,1024]{2,1,0:T(8,128)}, u32[]{:S(2)}) copy-start(f32[2,1024,1024]{2,1,0:T(8,128)} %refs_8_.1) | copy-start | bytes 25165828
where the time goes:
time: 816 us
  Pallas kernels  763 us (94%)
  other arithmetic  36.8 us (5%)
  waiting for transfers between devices  8.48 us (1%)
    pallas_call x1, Pallas kernels, step(): pl.pallas_call(functools.partial(kernel, lay), out_shape=[jax.ShapeDtypeS...  731 us
    add x2, other arithmetic, step(): new_v.append(0.95 * one_v + 0.05 * g * g)  36.8 us
    pallas_call x1, Pallas kernels, step(): pl.pallas_call(functools.partial(settle, lay), out_shape=[jax.ShapeDtypeS...  27.9 us
  transfers between devices with their start and end apart: 4, of which 2 were waited for; matrix products, arithmetic and copies ran while one was open for 5% of the time, Pallas kernels for 4%

commit v1 on v0

--- a/solution.py
+++ b/solution.py
@@ -14,7 +14,9 @@
 STRIP = 32
 LATER = 4
 LAST = 1
-PAUSE = 96
+OWN = 8
+AHEAD = 4
+PAUSE = 144
 FLIGHT = 32
 VMEM_LIMIT = 67043328
 
@@ -93,15 +95,17 @@
         i, layer = units[u]
         return lay[i].tile(arrays[i], layer, owner, h, t)
 
-    def first(d, i):
-        return remote(lay[i].of(grads[i], slice(None), across, d), hop[i].at[d], s1_send, s1_recv, d, i)
-
-    def plain(d, i):
-        src = lay[i].of(grads[i], slice(None), to[d], 1 - d)
-        return remote(src, got[i].at[d, 1 - d], s2_send, s2_recv, d, 2 * i + 1 - d)
-
-    def added(d, i):
-        return remote(hop[i].at[d], got[i].at[d, d], s2_send, s2_recv, d, 2 * i + d)
+    def first(d, u):
+        i, layer = units[u]
+        return remote(part(grads, u, across, d), hop[i].at[d, layer], s1_send, s1_recv, d, u)
+
+    def plain(d, u):
+        i, layer = units[u]
+        return remote(part(grads, u, to[d], 1 - d), got[i].at[d, 1 - d, layer], s2_send, s2_recv, d, 2 * u + 1 - d)
+
+    def added(d, u):
+        i, layer = units[u]
+        return remote(hop[i].at[d, layer], got[i].at[d, d, layer], s2_send, s2_recv, d, 2 * u + d)
 
     def out(d, u):
         i, layer = units[u]
@@ -116,16 +120,16 @@
     for device in to:
         pl.semaphore_signal(barrier, inc=1, device_id=(rep, device), device_id_type=MESH)
 
-    adds = [(d, u, t) for i in range(3) for d in ways for u in many if units[u][0] == i for t in range(tiles)]
+    adds = [(d, u, t) for u in many for d in ways for t in range(tiles)]
     steps = [(u, h, t) for u in many for h in range(2) for t in range(tiles)]
 
     def own_load(k):
         d, u, t = adds[k]
-        return pltpu.make_async_copy(tile(grads, u, to[d], d, t), own_b.at[k % 2], own_sem.at[k % 2])
+        return pltpu.make_async_copy(tile(grads, u, to[d], d, t), own_b.at[k % OWN], own_sem.at[k % OWN])
 
     def loads(k):
         u, h, t = steps[k]
-        s = k % 2
+        s = k % AHEAD
         pairs = ((tile(grads, u, me, h, t), g_b), (tile(weights, u, me, h, t), w_b), (tile(ms, u, 0, h, t), m_b), (tile(vs, u, 0, h, t), v_b))
         return [pltpu.make_async_copy(src, dst.at[s], in_sem.at[a, s]) for a, (src, dst) in enumerate(pairs)]
 
@@ -137,9 +141,11 @@
         u, h, t = steps[k]
         return pltpu.make_async_copy(sum_b.at[k % 2], tile(sums, u, 0, h, t), out_sem.at[1, k % 2])
 
-    own_load(0).start()
-    for copy in loads(0):
-        copy.start()
+    for k in range(OWN):
+        own_load(k).start()
+    for k in range(AHEAD):
+        for copy in loads(k):
+            copy.start()
 
     pl.semaphore_wait(barrier, 2)
 
@@ -148,31 +154,31 @@
         @pl.loop(0, PAUSE * (ROWS // STRIP))
         def _(turn):
             at = pl.ds(pl.multiple_of(lax.rem(turn, ROWS // STRIP) * STRIP, STRIP), STRIP)
-            m_b[1, at, :] = jnp.zeros((STRIP, COLS), jnp.float32)
-
-    for i in range(3):
+            sum_b[0, at, :] = jnp.zeros((STRIP, COLS), jnp.bfloat16)
+
+    for u in many:
         for d in ways:
-            first(d, i).start()
-    for i in range(3):
+            first(d, u).start()
+    for u in many:
         for d in ways:
-            plain(d, i).start()
+            plain(d, u).start()
 
     for k, (d, u, t) in enumerate(adds):
         i, layer = units[u]
-        if k + 1 < len(adds):
-            own_load(k + 1).start()
+        if t == 0:
+            first(d, u).wait_recv()
         own_load(k).wait()
-        if layer == t == 0:
-            first(d, i).wait_recv()
 
         @pl.loop(0, ROWS // STRIP)
         def _(strip, d=d, i=i, layer=layer, t=t, k=k):
             at = pl.ds(pl.multiple_of(strip * STRIP, STRIP), STRIP)
             there = (d, layer, *lay[i].inside(t, strip))
-            hop[i][there] = (hop[i][there].astype(jnp.float32) + own_b[k % 2, at, :].astype(jnp.float32)).astype(jnp.bfloat16)
-
-        if layer == lay[i].layers - 1 and t == tiles - 1:
-            added(d, i).start()
+            hop[i][there] = (hop[i][there].astype(jnp.float32) + own_b[k % OWN, at, :].astype(jnp.float32)).astype(jnp.bfloat16)
+
+        if t == tiles - 1:
+            added(d, u).start()
+        if k + OWN < len(adds):
+            own_load(k + OWN).start()
 
     def send_out(k):
         u, h, t = steps[k]
@@ -184,28 +190,28 @@
     for k, (u, h, t) in enumerate(steps):
         s = k % 2
         i, layer = units[u]
-        if k + 1 < len(steps):
-            for copy in loads(k + 1):
-                copy.start()
+        if t == 0:
+            for d in ways:
+                (added if d == h else plain)(d, u).wait_recv()
         for copy in loads(k):
             copy.wait()
-        if layer == t == 0:
-            for d in ways:
-                (added if d == h else plain)(d, i).wait_recv()
         if k >= 2:
             store_sum(k - 2).wait()
 
         @pl.loop(0, ROWS // STRIP)
-        def _(strip, s=s, i=i, layer=layer, h=h, t=t):
+        def _(strip, s=s, a=k % AHEAD, i=i, layer=layer, h=h, t=t):
             at = pl.ds(pl.multiple_of(strip * STRIP, STRIP), STRIP)
             there = (h, layer, *lay[i].inside(t, strip))
-            g = g_b[s, at, :].astype(jnp.float32) + got[i][(RIGHT, *there)].astype(jnp.float32)
+            g = g_b[a, at, :].astype(jnp.float32) + got[i][(RIGHT, *there)].astype(jnp.float32)
             g = (g + got[i][(LEFT, *there)].astype(jnp.float32)).astype(jnp.bfloat16)
             sum_b[s, at, :] = g
-            new_b[s, at, :] = adamw(w_b[s, at, :].astype(jnp.float32), m_b[s, at, :], v_b[s, at, :], g.astype(jnp.float32))[0]
+            new_b[s, at, :] = adamw(w_b[a, at, :].astype(jnp.float32), m_b[a, at, :], v_b[a, at, :], g.astype(jnp.float32))[0]
 
         store_new(k).start()
         store_sum(k).start()
+        if k + AHEAD < len(steps):
+            for copy in loads(k + AHEAD):
+                copy.start()
         if k >= 1:
             send_out(k - 1)
     end = len(steps) - 1
@@ -229,9 +235,9 @@
         dst = onward[d].at[to_k] if to_k < split else onward[2 + d].at[to_k - split]
         return pltpu.make_async_copy(src, dst, put_sem.at[k % 2, t])
 
-    for i in range(3):
+    for u in many:
         for d in ways:
-            added(d, i).wait_send()
+            added(d, u).wait_send()
     for k in range(len(later) + 2):
         if k < len(later):
             u, d = later[k]
@@ -250,10 +256,9 @@
             on(d, u).start()
 
     for d in ways:
-        for i in range(3):
-            first(d, i).wait_send()
-            plain(d, i).wait_send()
         for u in many:
+            first(d, u).wait_send()
+            plain(d, u).wait_send()
             out(d, u).wait_send()
             if u >= LATER:
                 on(d, u).wait()
@@ -333,18 +338,18 @@
             scratch_shapes=[
                 *(pltpu.VMEM((2, one.layers, *one.half), bf16) for one in lay),
                 *(pltpu.VMEM((2, 2, one.layers, *one.half), bf16) for one in lay),
+                pltpu.VMEM((OWN, ROWS, COLS), bf16),
+                pltpu.VMEM((AHEAD, ROWS, COLS), bf16),
+                pltpu.VMEM((AHEAD, ROWS, COLS), bf16),
+                pltpu.VMEM((AHEAD, ROWS, COLS), jnp.float32),
+                pltpu.VMEM((AHEAD, ROWS, COLS), jnp.float32),
                 pltpu.VMEM((2, ROWS, COLS), bf16),
                 pltpu.VMEM((2, ROWS, COLS), bf16),
-                pltpu.VMEM((2, ROWS, COLS), bf16),
-                pltpu.VMEM((2, ROWS, COLS), jnp.float32),
-                pltpu.VMEM((2, ROWS, COLS), jnp.float32),
-                pltpu.VMEM((2, ROWS, COLS), bf16),
-                pltpu.VMEM((2, ROWS, COLS), bf16),
-                dma((2, 3)), dma((2, 3)),
-                dma((2, 6)), dma((2, 6)),
+                dma((2, units)), dma((2, units)),
+                dma((2, 2 * units)), dma((2, 2 * units)),
                 dma((2, units)), dma((2, units)),
                 dma((2, units)), dma((2, units)),
-                dma((2,)), dma((4, 2)), dma((2, 2)), dma((2, tiles)),
+                dma((OWN,)), dma((4, AHEAD)), dma((2, 2)), dma((2, tiles)),
             ],
             compiler_params=pltpu.CompilerParams(collective_id=0, has_side_effects=True, vmem_limit_bytes=VMEM_LIMIT),
             name="sum_step_gather",

time: 816 us -> 816 us (level)
  no operation moved by 1% of the time
where the time goes in v1:
time: 816 us
  Pallas kernels  764 us (94%)
  other arithmetic  36.8 us (5%)
  waiting for transfers between devices  8.29 us (1%)
    pallas_call x1, Pallas kernels, step(): pl.pallas_call(functools.partial(kernel, lay), out_shape=[jax.ShapeDtypeS...  732 us
    add x2, other arithmetic, step(): new_v.append(0.95 * one_v + 0.05 * g * g)  36.8 us
    pallas_call x1, Pallas kernels, step(): pl.pallas_call(functools.partial(settle, lay), out_shape=[jax.ShapeDtypeS...  27.9 us
  transfers between devices with their start and end apart: 4, of which 2 were waited for; matrix products, arithmetic and copies ran while one was open for 5% of the time, Pallas kernels for 4%

profile of v1, /device:TPU:112, one launch (start us, length us, event | category | flops | bytes accessed | tf_op | source)
XLA Modules:
  0.0 815.9 jit_solution(12846262748498934497)
XLA Ops:
  0.6 731.6 %sum_step_gather.1 = (bf16[2,256,4096]{2,1,0:T(8,128)(2,1)}, bf16[2,256,4096]{2,1,0:T(8,128)(2,1)}, bf16[2,1024,1024]{2,1,0:T(8,128)(2,1)}, bf16[2,1024,4096]{2,...) custom-call(bf16[2,1024,4096]{2,1,0:T(8,128)(2,1)} %bitcast.3, ...), custom_call_target="tpu_custom_call" | custom-call | tf_op jit(solution)/shard_map/sum_step_gather/pallas_call | solution.py:330
  732.3 2.6 collective-permute-start.2
  734.8 0.8 collective-permute-start.3
  735.6 1.3 collective-permute-start
  736.8 2.0 collective-permute-start.1
  738.8 0.0 copy-start
  738.8 26.4 %fusion.3 = (f32[2,256,4096]{2,1,0:T(8,128)}, f32[2,256,4096]{2,1,0:T(8,128)}, f32[2,256,4096]{2,1,0:T(8,128)}, f32[2,256,4096]{2,1,0:T(8,128)}) fusion(bf16[2,256,4096]{2,1,0:T(8,128)(2,1)} %get-tuple-element.44, f32[2,256,4096]{2,1,0:T(8,128)} %refs_9_.1, f32[2,256,4096]{2,1,0:T(8,128)} %refs_6_.1, bf16[2,256,4096]{2,1,0:T(8,128)(2,1)} %get-tuple-element.45, ...), kind=kLoop, calls=%fused_computation.9 | loop fusion | flops 33554432 | bytes 75497472 | tf_op jit(solution)/shard_map/add | solution.py:378
  765.2 0.0 copy-done
  765.2 10.4 %fusion.5 = (f32[2,1024,1024]{2,1,0:T(8,128)}, f32[2,1024,1024]{2,1,0:T(8,128)}) fusion(bf16[2,1024,1024]{2,1,0:T(8,128)(2,1)} %get-tuple-element.46, f32[2,1024,1024]{2,1,0:T(8,128)} %refs_11_.1, f32[2,1024,1024]{2,1,0:T(8,128)S(1)} %copy-done), kind=kLoop, calls=%fused_computation.11 | loop fusion | flops 16777216 | bytes 37748736 | tf_op jit(solution)/shard_map/add | solution.py:378
  775.7 27.9 %settle.1 = (bf16[2,1024,4096]{2,1,0:T(8,128)(2,1)}, bf16[2,1024,4096]{2,1,0:T(8,128)(2,1)}, bf16[2,4096,1024]{2,1,0:T(8,128)(2,1)}) custom-call(bf16[2,1024,4096]{2,1,0:T(8,128)(2,1)} %get-tuple-element.32.refs_0_, bf16[2,1024,4096]{2,1,0:T(8,128)(2,1)} %get-tuple-element.33.refs_1_, bf16[2,4096,1024]{2,1,0:T(8,128)(2,1)} %get-tuple-element.34.refs_2_), custom_call_target="tpu_custom_call" | custom-call | flops 1006632960 | bytes 100663296 | tf_op jit(solution)/shard_map/settle/pallas_call | solution.py:364
  803.5 5.8 collective-permute-done.2.refs_0_
  809.3 0.0 collective-permute-done.3.refs_1_
  809.3 3.1 spread.2
  812.4 2.5 collective-permute-done.refs_0_
  814.9 0.0 collective-permute-done.1.refs_1_
  814.9 1.0 spread.3
Async XLA Ops:
  732.3 77.0 %collective-permute-start.2 = (bf16[7,256,1024]{2,1,0:T(8,128)(2,1)}, bf16[7,256,1024]{2,1,0:T(8,128)(2,1)S(1)}, u32[]{:S(2)}, u32[]{:S(2)}) collective-permute-start(bf16[7,256,1024]{2,1,0:T(8,128)(2,1)} %get-tuple-element.30), channel_id=1, source_target_pairs={{0,1},{1,2},{2,3},{3,0},{4,5},{5,6},{6,7},{7,4},{8,9},{9,10},{10,1... | collective-permute-start | bytes 11010056 | tf_op jit(solution)/shard_map/ppermute | solution.py:362
  734.8 74.5 %collective-permute-start.3 = (bf16[7,256,1024]{2,1,0:T(8,128)(2,1)}, bf16[7,256,1024]{2,1,0:T(8,128)(2,1)S(1)}, u32[]{:S(2)}, u32[]{:S(2)}) collective-permute-start(bf16[7,256,1024]{2,1,0:T(8,128)(2,1)} %get-tuple-element.31), channel_id=1, source_target_pairs={{0,3},{1,0},{2,1},{3,2},{4,7},{5,4},{6,5},{7,6},{8,11},{9,8},{10,9... | collective-permute-start | bytes 11010056 | tf_op jit(solution)/shard_map/ppermute | solution.py:362
  735.6 79.3 %collective-permute-start = (bf16[1,256,1024]{2,1,0:T(8,128)(2,1)}, bf16[1,256,1024]{2,1,0:T(8,128)(2,1)S(1)}, u32[]{:S(2)}, u32[]{:S(2)}) collective-permute-start(bf16[1,256,1024]{2,1,0:T(8,128)(2,1)} %get-tuple-element.28), channel_id=1, source_target_pairs={{0,1},{1,2},{2,3},{3,0},{4,5},{5,6},{6,7},{7,4},{8,9},{9,10},{10,1... | collective-permute-start | bytes 1572872 | tf_op jit(solution)/shard_map/ppermute | solution.py:362
  736.8 78.1 %collective-permute-start.1 = (bf16[1,256,1024]{2,1,0:T(8,128)(2,1)}, bf16[1,256,1024]{2,1,0:T(8,128)(2,1)S(1)}, u32[]{:S(2)}, u32[]{:S(2)}) collective-permute-start(bf16[1,256,1024]{2,1,0:T(8,128)(2,1)} %get-tuple-element.29), channel_id=1, source_target_pairs={{0,3},{1,0},{2,1},{3,2},{4,7},{5,4},{6,5},{7,6},{8,11},{9,8},{10,9... | collective-permute-start | bytes 1572872 | tf_op jit(solution)/shard_map/ppermute | solution.py:362
  738.8 26.4 %copy-start = (f32[2,1024,1024]{2,1,0:T(8,128)S(1)}, f32[2,1024,1024]{2,1,0:T(8,128)}, u32[]{:S(2)}) copy-start(f32[2,1024,1024]{2,1,0:T(8,128)} %refs_8_.1) | copy-start | bytes 25165828
